TPU v7x, 32 devices: a whole 2x2x4 slice. The times are simulated.
32 devices in a mesh: ta: 2 (over x), gz: 4 (over y, core), gy: 4 (over z).
Axes of the slice: x: 2, y: 2, z: 4, core: 2. Of those that a mesh axis runs over, the one named last changes fastest.
Arguments:
- propagator: bfloat16 [2, 4, 3, 12, 2, 4, 512], P(None, None, None, None, 'ta', 'gz', 'gy'), may hold values from -6 to 6
- links: bfloat16 [2, 3, 3, 2, 4, 512], P(None, None, None, 'ta', 'gz', 'gy'), may hold values from -2.5 to 2.5
- source_z: int32 [2, 4], replicated, may hold values from 0 to 3
- displacements: int32 [3], replicated, may hold values from 0 to 2, each once
- momenta: int32 [4], replicated, may hold values from 1 to 3
- gamma_perm: int32 [4, 4], replicated, may hold values from 0 to 3, each once within a row
- gamma_phase: int32 [4, 4], replicated, may hold values from 0 to 3
Outputs:
- correlator: float32 [2, 3, 4, 4, 2], replicated
Inputs may be any that keep to these rules, and one draw needn't show every extreme that they name: `displacements`: every displacement from -1 to 1 appears exactly once. `gamma_perm`: each row is a permutation of the four spin indices.
All inputs are finite; a program needn't handle non-finite values.
Results may differ from a plain program's by a relative error of at most 0.0003.
Values may be sent and summed in bfloat16 or wider, within the bound.
A program may use at most 64 MiB of HBM per device.

v0:
```python
import math
import jax
import jax.numpy as jnp
from jax import lax
from jax.sharding import PartitionSpec as P

highest = lax.Precision.HIGHEST


def from_behind(array, axis, by):
    peers = lax.axis_size(axis)
    return lax.ppermute(array, axis, [(i, (i + by) % peers) for i in range(peers)])


def colour_apply(wilson, field_now):
    left_real = wilson[0][None, :, :, None, :]
    left_imag = wilson[1][None, :, :, None, :]
    right_real = field_now[0][:, None, :, :, :]
    right_imag = field_now[1][:, None, :, :, :]
    real_part = jnp.sum(left_real * right_real - left_imag * right_imag, axis=2)
    imag_part = jnp.sum(left_real * right_imag + left_imag * right_real, axis=2)
    return jnp.stack([real_part, imag_part])


def link_product(left_link, right_link):
    left_real = left_link[0][:, :, None, :]
    left_imag = left_link[1][:, :, None, :]
    right_real = right_link[0][None, :, :, :]
    right_imag = right_link[1][None, :, :, :]
    real_part = jnp.sum(left_real * right_real - left_imag * right_imag, axis=1)
    imag_part = jnp.sum(left_real * right_imag + left_imag * right_real, axis=1)
    return jnp.stack([real_part, imag_part])


def spin_pairs(source, field_now):
    source_real = source[0][:, None]
    source_imag = source[1][:, None]
    field_real = field_now[0][None]
    field_imag = field_now[1][None]
    real_part = jnp.sum(source_real * field_real + source_imag * field_imag, axis=(2, 3))
    imag_part = jnp.sum(source_real * field_imag - source_imag * field_real, axis=(2, 3))
    return (real_part, imag_part)


def site_traces(gamma_real, gamma_imag, pairs):
    pair_real, pair_imag = pairs
    table_real = gamma_real[:, :, :, None]
    table_imag = gamma_imag[:, :, :, None]
    real_part = jnp.sum(table_real * pair_real[None] - table_imag * pair_imag[None], axis=(1, 2))
    imag_part = jnp.sum(table_real * pair_imag[None] + table_imag * pair_real[None], axis=(1, 2))
    return (real_part, imag_part)


def gamma_tables(gamma_perm, gamma_phase):
    columns = jnp.arange(4, dtype=jnp.int32)
    hits = (gamma_perm[:, :, None] == columns[None, None, :]).astype(jnp.float32)
    real_part = (gamma_phase == 0).astype(jnp.float32) - (gamma_phase == 2).astype(jnp.float32)
    imag_part = (gamma_phase == 1).astype(jnp.float32) - (gamma_phase == 3).astype(jnp.float32)
    return (hits * real_part[:, :, None], hits * imag_part[:, :, None])


def body(propagator, links, source_z, displacements, momenta, gamma_perm, gamma_phase):
    gamma_real, gamma_imag = gamma_tables(gamma_perm, gamma_phase)
    adjoint_real = jnp.swapaxes(gamma_real, 1, 2)
    adjoint_imag = -jnp.swapaxes(gamma_imag, 1, 2)
    depth_count = lax.axis_size("gz")
    nsteps = (displacements.shape[0] - 1) // 2
    slices_dev = propagator.shape[4]
    sites_dev = propagator.shape[6]
    slices_all = slices_dev * lax.axis_size("ta")
    sites_total = sites_dev * lax.axis_size("gy") * depth_count
    scaling = 1.0 / (24.0 * math.sqrt(sites_total))
    field_data, link_data = (propagator, links)
    depth_local = 1
    depth_start = lax.axis_index("gz")
    block_sites = field_data.shape[-1]
    line_length = depth_local * block_sites
    flat_length = slices_dev * line_length
    field_flat = jnp.reshape(field_data, (2, 4, 3, 12, flat_length))
    links_flat = jnp.reshape(link_data, (2, 3, 3, flat_length))
    positions = jnp.arange(flat_length, dtype=jnp.int32)
    depth_flat = depth_start + positions // block_sites % depth_local
    slice_flat = lax.axis_index("ta") * slices_dev + positions // line_length
    slice_ids = jnp.arange(slices_all, dtype=jnp.int32)
    slice_hits = slice_ids[:, None] == slice_flat[None, :]
    source_flat = jnp.sum(jnp.where(slice_hits[:, None, :], source_z[:, :, None], 0), axis=0)
    turn_count = momenta[:, None] * (depth_flat[None, :] - source_flat) % depth_count
    angles = turn_count.astype(jnp.float32) * (2.0 * math.pi / depth_count)
    cosine = jnp.cos(angles)
    sine_table = jnp.sin(angles)
    slice_weight = slice_hits.astype(jnp.float32)

    def contract(trace, table):
        return jnp.einsum("tl,gl,pl->tgp", slice_weight, trace, table, precision=highest)

    def project(traces):
        trace_real, trace_imag = traces
        real_part = contract(trace_real, cosine) + contract(trace_imag, sine_table)
        imag_part = contract(trace_imag, cosine) - contract(trace_real, sine_table)
        return jnp.stack([real_part, imag_part], axis=-1) * scaling

    source = field_flat.astype(jnp.float32)
    unit = jnp.broadcast_to(jnp.eye(3, dtype=jnp.float32)[:, :, None], (3, 3, flat_length))
    identity = jnp.stack([unit, jnp.zeros_like(unit)])
    results = {0: project(site_traces(gamma_real, gamma_imag, spin_pairs(source, source)))}
    wilson = identity
    moved_field = field_flat
    moved_links = links_flat
    for reach in range(1, nsteps + 1):
        wilson = link_product(wilson, moved_links.astype(jnp.float32))
        moved_field, moved_links = from_behind((moved_field, moved_links), "gz", -1)
        pairs = spin_pairs(source, colour_apply(wilson, moved_field.astype(jnp.float32)))
        results[reach] = project(site_traces(gamma_real, gamma_imag, pairs))
        mirrored_trace_real, mirrored_trace_imag = site_traces(adjoint_real, adjoint_imag, pairs)
        other_real = contract(mirrored_trace_real, cosine) - contract(
            mirrored_trace_imag, sine_table
        )
        other_imag = contract(mirrored_trace_imag, cosine) + contract(
            mirrored_trace_real, sine_table
        )
        shift_turn = momenta * reach % depth_count
        shift_angle = shift_turn.astype(jnp.float32) * (2.0 * math.pi / depth_count)
        shift_cos = jnp.cos(shift_angle)
        shift_sin = jnp.sin(shift_angle)
        mirrored_real_part = other_real * shift_cos - other_imag * shift_sin
        mirrored_imag_part = -other_imag * shift_cos - other_real * shift_sin
        results[-reach] = jnp.stack([mirrored_real_part, mirrored_imag_part], axis=-1) * scaling
    stacked = jnp.stack([results[offset] for offset in range(-nsteps, nsteps + 1)], axis=1)
    offsets = jnp.arange(2 * nsteps + 1, dtype=jnp.int32)
    select = (displacements[:, None] == offsets[None, :]).astype(jnp.float32)
    ordered = jnp.einsum("jl,tlgpc->tjgpc", select, stacked, precision=highest)
    return lax.psum(ordered, ("ta", "gz", "gy"))


def solution(mesh):
    placed = (
        P(None, None, None, None, "ta", "gz", "gy"),
        P(None, None, None, "ta", "gz", "gy"),
        P(),
        P(),
        P(),
        P(),
        P(),
    )
    return jax.shard_map(body, mesh=mesh, in_specs=placed, out_specs=P(), check_vma=False)
```

profile of v0, /device:TPU:0, one launch (start us, length us, event | category | flops | bytes accessed | tf_op | source)
XLA Modules:
  0.0 51.4 jit_solution(15262922463979435672)
XLA Ops:
  0.0 2.4 %collective-permute-start = (bf16[2,4,3,12,128]{4,1,3,2,0:T(4,128)(2,1)}, bf16[2,4,3,12,128]{4,1,3,2,0:T(4,128)(2,1)S(1)}, u32[]{:S(2)}, u32[]{:S(2)}) collective-permute-start(bf16[2,4,3,12,128]{4,1,3,2,0:T(4,128)(2,1)} %bitcast.123), channel_id=1, source_target_pairs={{0,12},{4,0},{8,4},{12,8},{1,13},{5,1},{9,5},{13,9},{2,14},{6,2},{... | collective-permute-start | bytes 221192 | tf_op jit(solution)/shard_map/ppermute | solution.py:12
  2.4 0.7 %copy_convert_fusion = f32[2,3,3,1,1,128]{5,2,1,4,3,0:T(4,128)S(1)} fusion(bf16[2,3,3,1,1,128]{5,0,4,3,2,1:T(2,128)(2,1)} %param.8), kind=kLoop, calls=%fused_computation.41 | loop fusion | flops 2304 | bytes 13824 | tf_op jit(solution)/shard_map/convert_element_type | solution.py:110
  3.1 0.9 %bitcast_convert_fusion = f32[2,4,3,12,128]{4,1,3,2,0:T(4,128)S(1)} fusion(bf16[2,4,3,12,1,1,128]{6,1,5,4,3,2,0:T(4,128)(2,1)} %param.7), kind=kLoop, calls=%fused_computation.140 | loop fusion | flops 36864 | bytes 221184 | tf_op jit(solution)/shard_map/convert_element_type | solution.py:102
  4.1 0.0 copy-start.1
  4.1 0.7 %copy-done.1 = s32[4,4]{1,0:T(4,128)S(1)} copy-done((s32[4,4]{1,0:T(4,128)S(1)}, s32[4,4]{1,0:T(4,128)}, u32[]{:S(2)}) %copy-start.1) | copy-done | bytes 88
  4.8 0.0 copy-start.3
  4.8 0.6 %copy-done.3 = s32[4]{0:T(128)S(1)} copy-done((s32[4]{0:T(128)S(1)}, s32[4]{0:T(128)}, u32[]{:S(2)}) %copy-start.3) | copy-done | bytes 40
  5.5 0.0 copy-start.2
  5.5 0.7 %copy-done.2 = s32[2,4]{1,0:T(2,128)S(1)} copy-done((s32[2,4]{1,0:T(2,128)S(1)}, s32[2,4]{1,0:T(2,128)}, u32[]{:S(2)}) %copy-start.2) | copy-done | bytes 56
  6.2 0.1 select_reduce_fusion
  6.3 0.1 fusion.88
  6.5 0.0 copy-start
  6.5 0.7 %copy-done = s32[4,4]{1,0:T(4,128)S(1)} copy-done((s32[4,4]{1,0:T(4,128)S(1)}, s32[4,4]{1,0:T(4,128)}, u32[]{:S(2)}) %copy-start) | copy-done | bytes 88
  7.2 0.1 fusion.6
  7.2 0.1 subtract_reduce_fusion.6
  7.3 0.0 collective-permute-done
  7.4 0.2 subtract_reduce_fusion.2
  7.6 0.4 add_reduce_fusion
  8.0 0.2 add_reduce_fusion.5
  8.1 0.2 fusion.24
  8.3 0.2 fusion.18
  8.5 0.2 convolution_add_fusion.1
  8.6 0.2 convolution_subtract_fusion.1
  8.8 0.2 fusion.34
  9.0 0.2 fusion.28
  9.1 0.2 convolution_subtract_fusion.2
  9.3 0.2 fusion.14
  9.4 0.2 fusion.8
  9.6 0.2 convolution_add_fusion
  9.8 0.2 convolution_subtract_fusion
  10.0 0.2 multiply_subtract_fusion.1
  10.2 0.0 copy-start.4
  10.2 0.6 %copy-done.4 = s32[3]{0:T(128)S(1)} copy-done((s32[3]{0:T(128)S(1)}, s32[3]{0:T(128)}, u32[]{:S(2)}) %copy-start.4) | copy-done | bytes 36
  10.8 0.2 convolution_bitcast_fusion
  11.1 39.7 %psum.7 = f32[2,3,4,4,2]{3,1,4,2,0:T(4,128)S(1)} all-reduce(f32[2,3,4,4,2]{3,1,4,2,0:T(4,128)S(1)} %convolution_bitcast_fusion), channel_id=1, replica_groups=mesh['ta'=2,'gz'=4,'gy'=4] {'ta','gz','gy'}, use_global_device_ids=true, to_apply=%region_15.16 | all-reduce | flops 192 | bytes 1536 | tf_op jit(solution)/shard_map/psum | solution.py:132
  50.8 0.6 %copy.45 = f32[2,3,4,4,2]{3,4,2,1,0:T(2,128)} copy(f32[2,3,4,4,2]{3,1,4,2,0:T(4,128)S(1)} %psum.7) | data formatting | bytes 1536 | tf_op jit(solution)/shard_map/psum | solution.py:132
  (16 shorter events, 0.3 us)
Async XLA Ops:
  0.0 7.3 %collective-permute-start = (bf16[2,4,3,12,128]{4,1,3,2,0:T(4,128)(2,1)}, bf16[2,4,3,12,128]{4,1,3,2,0:T(4,128)(2,1)S(1)}, u32[]{:S(2)}, u32[]{:S(2)}) collective-permute-start(bf16[2,4,3,12,128]{4,1,3,2,0:T(4,128)(2,1)} %bitcast.123), channel_id=1, source_target_pairs={{0,12},{4,0},{8,4},{12,8},{1,13},{5,1},{9,5},{13,9},{2,14},{6,2},{... | collective-permute-start | bytes 221192 | tf_op jit(solution)/shard_map/ppermute | solution.py:12
  4.1 0.7 %copy-start.1 = (s32[4,4]{1,0:T(4,128)S(1)}, s32[4,4]{1,0:T(4,128)}, u32[]{:S(2)}) copy-start(s32[4,4]{1,0:T(4,128)} %param.13) | copy-start | bytes 196
  4.8 0.7 %copy-start.3 = (s32[4]{0:T(128)S(1)}, s32[4]{0:T(128)}, u32[]{:S(2)}) copy-start(s32[4]{0:T(128)} %param.11) | copy-start | bytes 52
  5.5 0.7 %copy-start.2 = (s32[2,4]{1,0:T(2,128)S(1)}, s32[2,4]{1,0:T(2,128)}, u32[]{:S(2)}) copy-start(s32[2,4]{1,0:T(2,128)} %param.9) | copy-start | bytes 100
  6.5 0.7 %copy-start = (s32[4,4]{1,0:T(4,128)S(1)}, s32[4,4]{1,0:T(4,128)}, u32[]{:S(2)}) copy-start(s32[4,4]{1,0:T(4,128)} %param.12) | copy-start | bytes 196
  10.2 0.7 %copy-start.4 = (s32[3]{0:T(128)S(1)}, s32[3]{0:T(128)}, u32[]{:S(2)}) copy-start(s32[3]{0:T(128)} %param.10) | copy-start | bytes 40
where the time goes:
time: 51.7 us; the launch traced here: 51.4 us
  blocking collectives  39.7 us (77%)
  local copies, waits for them, and re-layouts  4.07 us (8%)
  other arithmetic  2.84 us (5%)
  starting transfers between devices  2.43 us (5%)
  matrix products  2.18 us (4%)
    psum x1, blocking collectives, body(): return lax.psum(ordered, ('ta', 'gz', 'gy'))  39.7 us
    unnamed x10, local copies, waits for them, and re-layouts  3.31 us
    ppermute x1, starting transfers between devices, from_behind(): lax.ppermute(array, axis, [(i, (i + by) % peers) for i in range(peers)])  2.43 us
    dot_general x12, matrix products, contract(): jnp.einsum('tl,gl,pl->tgp', slice_weight, trace, table, precision=highest)  1.96 us
  transfers between devices with their start and end apart: 1, of which 0 were waited for; matrix products, arithmetic and copies ran while one was open for 4% of the time, Pallas kernels for 0%

commit v1 on v0

--- a/solution.py
+++ b/solution.py
@@ -129,7 +129,7 @@
     offsets = jnp.arange(2 * nsteps + 1, dtype=jnp.int32)
     select = (displacements[:, None] == offsets[None, :]).astype(jnp.float32)
     ordered = jnp.einsum("jl,tlgpc->tjgpc", select, stacked, precision=highest)
-    return lax.psum(ordered, ("ta", "gz", "gy"))
+    return jnp.sum(lax.all_gather(ordered, ("ta", "gz", "gy")), axis=0)
 
 
 def solution(mesh):

time: 51.7 us -> 85.9 us (1.66)
  blocking collectives: 39.7 us -> 74.4 us
    all_gather x0 -> x1, blocking collectives: none -> 74.4 us  [body(): return jnp.sum(lax.all_gather(ordered, ('ta', 'gz', 'gy')), axis=0)]
    psum x1 -> x0, blocking collectives: 39.7 us -> none  [body(): return lax.psum(ordered, ('ta', 'gz', 'gy'))]
    unnamed x10 -> x12, local copies, waits for them, and re-layouts: 3.31 us -> 3.28 us
  transfers between devices with their start and end apart: 1 -> 1, of which waited for: 0 -> 0; matrix products, arithmetic and copies ran while one was open for 4% -> 2% of each run, Pallas kernels for 0% -> 0%
where the time goes in v1:
time: 85.9 us; the launch traced here: 85.6 us
  blocking collectives  74.4 us (87%)
  local copies, waits for them, and re-layouts  4.04 us (5%)
  starting transfers between devices  2.43 us (3%)
  other arithmetic  2.36 us (3%)
  matrix products  2.18 us (3%)
    all_gather x1, blocking collectives, body(): return jnp.sum(lax.all_gather(ordered, ('ta', 'gz', 'gy')), axis=0)  74.4 us
    unnamed x12, local copies, waits for them, and re-layouts  3.28 us
    ppermute x1, starting transfers between devices, from_behind(): lax.ppermute(array, axis, [(i, (i + by) % peers) for i in range(peers)])  2.43 us
    dot_general x12, matrix products, contract(): jnp.einsum('tl,gl,pl->tgp', slice_weight, trace, table, precision=highest)  1.96 us
  transfers between devices with their start and end apart: 1, of which 0 were waited for; matrix products, arithmetic and copies ran while one was open for 2% of the time, Pallas kernels for 0%

profile of v1, /device:TPU:0, one launch (start us, length us, event | category | flops | bytes accessed | tf_op | source)
XLA Modules:
  0.0 85.6 jit_solution(18145779641307969657)
XLA Ops:
  0.0 0.0 copy-start.1
  0.0 2.4 %collective-permute-start = (bf16[2,4,3,12,128]{4,1,3,2,0:T(4,128)(2,1)}, bf16[2,4,3,12,128]{4,1,3,2,0:T(4,128)(2,1)S(1)}, u32[]{:S(2)}, u32[]{:S(2)}) collective-permute-start(bf16[2,4,3,12,128]{4,1,3,2,0:T(4,128)(2,1)} %bitcast.125), channel_id=1, source_target_pairs={{0,12},{4,0},{8,4},{12,8},{1,13},{5,1},{9,5},{13,9},{2,14},{6,2},{... | collective-permute-start | bytes 221192 | tf_op jit(solution)/shard_map/ppermute | solution.py:12
  2.4 0.0 copy-done.1
  2.5 0.9 %bitcast_convert_fusion = f32[2,4,3,12,128]{4,1,3,2,0:T(4,128)S(1)} fusion(bf16[2,4,3,12,1,1,128]{6,1,5,4,3,2,0:T(4,128)(2,1)} %param.7), kind=kLoop, calls=%fused_computation.140 | loop fusion | flops 36864 | bytes 221184 | tf_op jit(solution)/shard_map/convert_element_type | solution.py:102
  3.4 0.0 copy-start.4
  3.5 0.6 copy-done.4
  4.2 0.0 copy-start.3
  4.2 0.7 copy-done.3
  4.9 0.1 select_reduce_fusion
  4.9 0.1 fusion.88
  5.1 0.0 copy-start.2
  5.1 0.6 copy-done.2
  5.8 0.0 copy-start
  5.8 0.7 copy-done
  6.5 0.1 fusion.6
  6.6 0.1 subtract_reduce_fusion.6
  6.7 0.0 collective-permute-done
  6.7 0.2 subtract_reduce_fusion.2
  6.9 0.4 add_reduce_fusion
  7.3 0.2 add_reduce_fusion.5
  7.5 0.2 fusion.34
  7.6 0.2 fusion.28
  7.8 0.2 fusion.8
  7.9 0.2 fusion.14
  8.1 0.2 convolution_subtract_fusion.2
  8.3 0.2 convolution_subtract_fusion
  8.4 0.2 convolution_add_fusion
  8.6 0.2 fusion.18
  8.8 0.2 fusion.24
  8.9 0.2 convolution_subtract_fusion.1
  9.1 0.2 convolution_add_fusion.1
  9.3 0.2 multiply_subtract_fusion.1
  9.5 0.0 copy-start.5
  9.5 0.6 copy-done.5
  10.2 0.2 convolution_bitcast_fusion
  10.4 74.4 %all-gather = f32[64,3,4,4,2]{3,2,4,1,0:T(4,128)S(1)} all-gather(f32[2,3,4,4,2]{3,2,4,1,0:T(4,128)S(1)} %copy.59), channel_id=2, replica_groups=mesh['ta'=2,'gz'=4,'gy'=4] {'ta','gz','gy'}, dimensions={0}, use_global_device_ids=true | all-gather | bytes 25344 | tf_op jit(solution)/shard_map/all_gather | solution.py:132
  84.8 0.2 reduce_sum.177
  85.0 0.6 copy.61
  (18 shorter events, 0.3 us)
Async XLA Ops:
  0.0 2.4 %copy-start.1 = (bf16[2,3,3,1,1,128]{5,0,4,3,2,1:T(2,128)(2,1)S(1)}, bf16[2,3,3,1,1,128]{5,0,4,3,2,1:T(2,128)(2,1)}, u32[]{:S(2)}) copy-start(bf16[2,3,3,1,1,128]{5,0,4,3,2,1:T(2,128)(2,1)} %param.8) | copy-start | bytes 13828
  0.0 6.7 %collective-permute-start = (bf16[2,4,3,12,128]{4,1,3,2,0:T(4,128)(2,1)}, bf16[2,4,3,12,128]{4,1,3,2,0:T(4,128)(2,1)S(1)}, u32[]{:S(2)}, u32[]{:S(2)}) collective-permute-start(bf16[2,4,3,12,128]{4,1,3,2,0:T(4,128)(2,1)} %bitcast.125), channel_id=1, source_target_pairs={{0,12},{4,0},{8,4},{12,8},{1,13},{5,1},{9,5},{13,9},{2,14},{6,2},{... | collective-permute-start | bytes 221192 | tf_op jit(solution)/shard_map/ppermute | solution.py:12
  3.4 0.7 copy-start.4
  4.2 0.7 copy-start.3
  5.1 0.7 copy-start.2
  5.8 0.7 copy-start
  9.5 0.7 copy-start.5
